TPU v7x, 8 devices: a whole 2x2x1 slice. The times are simulated.
8 devices in a mesh: z: 2 (over z, y), y: 2 (over x), x: 2 (over core).
Axes of the slice: x: 2, y: 2, z: 1, core: 2. Of those that a mesh axis runs over, the one named last changes fastest.
Arguments:
- atom_pos: float32 [5832, 3], P(('z', 'y', 'x'))
- atom_vel: float32 [5832, 3], P(('z', 'y', 'x'))
- atom_frc: float32 [5832, 3], P(('z', 'y', 'x'))
- atom_id: int32 [5832], P(('z', 'y', 'x'))
- atom_ok: int32 [5832], P(('z', 'y', 'x'))
- brick_side: float32 [], replicated
Outputs:
- output 1: float32 [5832, 3], P(('z', 'y', 'x'))
- output 2: float32 [5832, 3], P(('z', 'y', 'x'))
- output 3: float32 [5832, 3], P(('z', 'y', 'x'))
- output 4: int32 [5832], P(('z', 'y', 'x'))
- output 5: int32 [5832], P(('z', 'y', 'x'))
- output 6: float32 [], replicated
All inputs are finite; a program needn't handle non-finite values.
Results may differ from a plain program's by a relative error of at most 0.001.
Values sent between devices are 32-bit elements.
A program may use at most 1 GiB of HBM per device.

v0:
```python
import functools

import jax
import jax.numpy as jnp
from jax import lax
from jax.experimental import pallas as pl
from jax.experimental.pallas import tpu as pltpu
from jax.sharding import PartitionSpec as P

DT = 0.005
RC = 2.5
FAR_AWAY = 1.0e6
UCUT = 4.0 * (RC ** -12 - RC ** -6)
UPC = -48.0 * RC ** -13 + 24.0 * RC ** -7
MESH_AXES = ("z", "y", "x")
CAP = 729
PAD = 768
MIG = 256
FULL = PAD + MIG
SEG = {1: (0, 16), 2: (16, 16), 4: (32, 16), 3: (48, 32), 5: (80, 32), 6: (128, 32), 7: (160, 64)}
IC = 32
NARROW = 512
FAR_FIRST = (6, 7, 4, 2, 5, 3, 1)
REACH = RC + 0.01
MESH_ID = pl.DeviceIdType.MESH


def pieces_of(rows):
    first = rows.astype(jnp.bfloat16).astype(jnp.float32)
    rest = rows - first
    second = rest.astype(jnp.bfloat16).astype(jnp.float32)
    third = rest - second
    return jnp.concatenate([first, second, third], axis=0).astype(jnp.bfloat16)


def select_rows(rows, onehot):
    out = lax.dot_general(pieces_of(rows), onehot, (((1,), (1,)), ((), ())), preferred_element_type=jnp.float32)
    return out[0:8] + out[8:16] + out[16:24]


def partner(relation):
    mine = (lax.axis_index("z"), lax.axis_index("y"), lax.axis_index("x"))
    bits = (relation // 4 % 2, relation // 2 % 2, relation % 2)
    return tuple((axis + bit) % 2 for axis, bit in zip(mine, bits))


def greet():
    barrier = pltpu.get_barrier_semaphore()
    for relation in range(1, 8):
        pl.semaphore_signal(barrier, inc=1, device_id=partner(relation), device_id_type=MESH_ID)
    return barrier


def axis_column(values, rows):
    idx = lax.broadcasted_iota(jnp.int32, (rows, 1), 0)
    out = jnp.full((rows, 1), values[-1], jnp.float32)
    for k in range(len(values) - 1):
        out = jnp.where(idx == k, values[k], out)
    return out


def brick_coords():
    return [lax.axis_index(name).astype(jnp.float32) for name in ("x", "y", "z")]


def prefix_counts(member):
    blocks = member.shape[1] // 128
    stacked = jnp.concatenate([member[:, 128 * b:128 * (b + 1)] for b in range(blocks)], axis=0).astype(jnp.bfloat16)
    row = lax.broadcasted_iota(jnp.int32, (128, 256), 0)
    col = lax.broadcasted_iota(jnp.int32, (128, 256), 1)
    ladder = ((row < col) | (col >= 128)).astype(jnp.float32).astype(jnp.bfloat16)
    counts = jnp.dot(stacked, ladder, preferred_element_type=jnp.float32)
    before = jnp.zeros((8, 128), jnp.float32)
    ranks = []
    for b in range(blocks):
        ranks.append(counts[8 * b:8 * b + 8, 0:128] + before)
        before = before + counts[8 * b:8 * b + 8, 128:256]
    return jnp.concatenate(ranks, axis=1), before


def exchange_kernel(pos_hbm, vel_hbm, frc_hbm, id_hbm, ok_hbm, side_hbm, own_ref, all_ref, mig_ref, pos_ref, vel_ref, frc_ref, id_ref, ok_ref, side_ref, pad_ref, load_sem, send_sem, recv_sem):
    loads = []
    for k, (src, dst) in enumerate(((pos_hbm, pos_ref), (vel_hbm, vel_ref), (frc_hbm, frc_ref), (id_hbm, id_ref), (ok_hbm, ok_ref), (side_hbm, side_ref))):
        load = pltpu.make_async_copy(src, dst, load_sem.at[k])
        load.start()
        loads.append(load)
    barrier = greet()
    pad_ref[...] = jnp.zeros_like(pad_ref)
    for load in loads:
        load.wait()
    side = side_ref[...]
    box = side * 2.0
    half_v = vel_ref[...] + (0.5 * DT) * frc_ref[...]
    pad_ref[0:3, 0:CAP] = pos_ref[...] + DT * half_v
    pad_ref[3:6, 0:CAP] = half_v
    pad_ref[6:7, 0:CAP] = (id_ref[...].reshape(1, CAP) >> 16).astype(jnp.float32) + 1.0
    pad_ref[7:8, 0:CAP] = (id_ref[...].reshape(1, CAP) & 65535).astype(jnp.float32)
    pad_ref[8:9, 0:CAP] = ok_ref[...].reshape(1, CAP).astype(jnp.float32)
    unwrapped = pad_ref[0:3, :]
    owned = pad_ref[8:9, :] > 0.5
    moved = jnp.where(unwrapped < 0.0, unwrapped + box, jnp.where(unwrapped >= box, unwrapped - box, unwrapped))
    for axis in range(3):
        all_ref[0, :, PAD * axis:PAD * (axis + 1)] = jnp.where(owned, moved[axis:axis + 1, :], FAR_AWAY)

    low = axis_column([coord * side for coord in brick_coords()], 3)
    outside = (unwrapped < low) | (unwrapped >= low + side)
    bits = jnp.where(outside, axis_column([1.0, 2.0, 4.0], 3), 0.0)
    code = jnp.sum(bits, axis=0, keepdims=True)
    code = jnp.where(owned, code, -1.0)
    relation_col = lax.broadcasted_iota(jnp.int32, (8, PAD), 0).astype(jnp.float32)
    member = code == relation_col
    rank, _ = prefix_counts(member.astype(jnp.float32))
    offset = axis_column([0.0] + [float(SEG[m][0]) for m in range(1, 8)], 8)
    slot = jnp.sum(jnp.where(member, rank + offset, 0.0), axis=0, keepdims=True)
    slot = jnp.where(code > 0.5, slot, -1.0)
    rows = jnp.concatenate([moved, pad_ref[3:8, :]], axis=0)
    slots = lax.broadcasted_iota(jnp.int32, (MIG, PAD), 0).astype(jnp.float32)
    onehot = (slots == slot).astype(jnp.float32).astype(jnp.bfloat16)
    mig_ref[0] = select_rows(rows, onehot)
    own_ref[0:8, :] = rows
    own_ref[8:9, :] = jnp.where(code == 0.0, rank[0:1, :], -1.0)
    own_ref[9:10, :] = jnp.broadcast_to(side, (1, PAD))

    pl.semaphore_wait(barrier, 7)
    copies = []
    for relation in FAR_FIRST:
        block = pl.ds(SEG[relation][0] // 128 * 128, 128)
        for which, src, dst in ((0, mig_ref.at[0, :, block], mig_ref.at[relation, :, block]), (1, all_ref.at[0], all_ref.at[relation])):
            copy = pltpu.make_async_remote_copy(src_ref=src, dst_ref=dst, send_sem=send_sem.at[which, relation], recv_sem=recv_sem.at[which, relation], device_id=partner(relation), device_id_type=MESH_ID)
            copy.start()
            copies.append(copy)
    for copy in copies:
        copy.wait()


def pair_terms(own, other, span):
    delta = []
    for mine, theirs in zip(own, other):
        diff = mine - theirs
        if span is not None:
            diff = diff - jnp.where(diff > 0.5 * span, span, jnp.where(diff < -0.5 * span, -span, 0.0))
        delta.append(diff)
    dist_sq = delta[0] * delta[0] + delta[1] * delta[1] + delta[2] * delta[2]
    in_range = (dist_sq < RC * RC) & (dist_sq > 0.01)
    inv_r = jnp.where(in_range, lax.rsqrt(dist_sq), 0.0)
    inv_r2 = inv_r * inv_r
    inv_r6 = inv_r2 * inv_r2 * inv_r2
    inv_r12 = inv_r6 * inv_r6
    well = inv_r12 - inv_r6
    scale = (well + inv_r12) * inv_r2 + (UPC / 24.0) * inv_r
    return [scale * d for d in delta], [well, dist_sq * inv_r, jnp.where(in_range, 1.0, 0.0)]


def force_kernel(own_ref, all_ref, mig_ref, en_ref, acc_ref, rows_ref, cand_ref, near_ref, mine_ref, plane_ref, list_ref, rank_ref, count_ref):
    side = own_ref[9:10, 0:1]
    box = side * 2.0
    lane = lax.broadcasted_iota(jnp.int32, (1, MIG), 1)
    arrivals = jnp.zeros((8, MIG), jnp.float32)
    for relation, (start, size) in SEG.items():
        arrivals = jnp.where((lane >= start) & (lane < start + size), mig_ref[relation], arrivals)
    cand_ref[:, 0:PAD] = own_ref[0:8, :]
    cand_ref[:, PAD:FULL] = arrivals
    stay_rank = own_ref[8:9, :]
    cand = cand_ref[...]
    valid = jnp.concatenate([stay_rank >= 0.0, arrivals[6:7, :] > 0.5], axis=1)
    total = jnp.sum(valid.astype(jnp.int32))
    tail = all_ref[0, :, NARROW:PAD]
    for relation in range(1, 8):
        tail = jnp.minimum(tail, all_ref[relation, :, NARROW:PAD])
    narrow = (jnp.min(tail) > 0.5 * FAR_AWAY) & (total <= NARROW)
    number = (cand[6:7, :].astype(jnp.int32) - 1) * 65536 + cand[7:8, :].astype(jnp.int32)
    key = jnp.where(valid, number, 2147483647)
    key_col = jnp.transpose(jnp.broadcast_to(key[:, PAD:FULL], (8, MIG)))[:, 0:1]
    below = (key_col < key).astype(jnp.float32).astype(jnp.bfloat16)
    in_front = jnp.dot(jnp.ones((8, MIG), jnp.bfloat16), below, preferred_element_type=jnp.float32)[0:1, :]
    above = lax.dot_general(jnp.ones((8, PAD), jnp.bfloat16), below[:, 0:PAD], (((1,), (1,)), ((), ())), preferred_element_type=jnp.float32)[0:1, :]
    rank = in_front + jnp.concatenate([stay_rank, float(PAD) - above], axis=1)
    rank_ref[...] = jnp.where(valid, rank, -1.0)
    centre = [(coord + 0.5) * side for coord in brick_coords()]

    def prepare(width):
        for relation in range(8):
            for axis in range(3):
                plane_ref[axis, relation:relation + 1, 0:width] = all_ref[relation, :, PAD * axis:PAD * axis + width]
        planes = []
        beyond = jnp.zeros((8, width), jnp.float32)
        for axis in range(3):
            theirs = plane_ref[axis, :, 0:width] - centre[axis]
            theirs = jnp.where(theirs > side, theirs - box, jnp.where(theirs < -side, theirs + box, theirs))
            excess = jnp.maximum(jnp.abs(theirs) - 0.5 * side, 0.0)
            beyond = beyond + excess * excess
            planes.append(theirs)
        keep = (beyond < REACH * REACH) & (beyond > 0.0)
        front, held = prefix_counts(keep.astype(jnp.float32))
        lanes = lax.broadcasted_iota(jnp.int32, (8, width), 1)
        hops = jnp.where(keep, lanes - front.astype(jnp.int32), 0)

        ranks = jnp.concatenate([rank_ref[:, 0:width], rank_ref[:, PAD:FULL]], axis=1)
        pieces = pieces_of(jnp.concatenate([cand_ref[:, 0:width], cand_ref[:, PAD:FULL]], axis=1))
        slots = lax.broadcasted_iota(jnp.int32, (128, width + MIG), 0).astype(jnp.float32)
        blocks = width // 128
        done = 0
        for bit in range(10 if width > 512 else 9):
            step = 1 << bit
            coming = pltpu.roll(hops, width - step, 1)
            take = (coming & step) != 0
            leave = (hops & step) != 0
            hops = jnp.where(take, coming, jnp.where(leave, 0, hops))
            planes = [jnp.where(take, pltpu.roll(plane, width - step, 1), plane) for plane in planes]
            if done < blocks:
                onehot = (slots == ranks - 128.0 * done).astype(jnp.float32).astype(jnp.bfloat16)
                out = lax.dot_general(pieces, onehot, (((1,), (1,)), ((), ())), preferred_element_type=jnp.float32)
                rows_ref[:, 128 * done:128 * done + 128] = out[0:8] + out[8:16] + out[16:24]
                done += 1
        if width < PAD:
            rows_ref[:, width:PAD] = jnp.zeros((8, PAD - width), jnp.float32)

        rows = rows_ref[:, 0:width]
        filled = rows[6:7, :] > 0.5
        local = rows[0:3, :] - axis_column(centre, 3)
        near_ref[0:3, 0:width] = jnp.where(filled, local, FAR_AWAY)
        local = jnp.concatenate([jnp.where(filled, local, -FAR_AWAY), jnp.zeros((5, width), jnp.float32)], axis=0)
        piece_row = lax.broadcasted_iota(jnp.int32, (24, 384), 0) % 8
        piece_col = lax.broadcasted_iota(jnp.int32, (24, 384), 1) // 128
        spread = (piece_row == piece_col).astype(jnp.float32).astype(jnp.bfloat16)
        columns = lax.dot_general(pieces_of(local), spread, (((0,), (0,)), ((), ())), preferred_element_type=jnp.float32)
        for axis in range(3):
            mine_ref[axis, 0:width, :] = columns[:, 128 * axis:128 * axis + 128]

        for relation in range(8):
            for axis in range(3):
                list_ref[relation, axis:axis + 1, 0:width] = planes[axis][relation:relation + 1, :]
        held = held.astype(jnp.int32)
        lane128 = lax.broadcasted_iota(jnp.int32, (8, 128), 1)
        start = total
        for relation in range(8):
            into = start % 128
            first = pl.multiple_of(start - into, 128)
            turned = pltpu.roll(list_ref[relation, :, 0:width + 128], into, 1)
            near_ref[:, pl.ds(first, 128)] = jnp.where(lane128 < into, near_ref[:, pl.ds(first, 128)], turned[:, 0:128])
            near_ref[:, pl.ds(pl.multiple_of(first + 128, 128), width)] = turned[:, 128:width + 128]
            start = start + held[relation, 0]
        into = start % 128
        first = pl.multiple_of(start - into, 128)
        near_ref[:, pl.ds(first, 128)] = jnp.where(lane128 < into, near_ref[:, pl.ds(first, 128)], FAR_AWAY)
        count_ref[0] = (start + 127) // 128

    @pl.when(narrow)
    def _():
        prepare(NARROW)

    @pl.when(jnp.logical_not(narrow))
    def _():
        prepare(PAD)

    n_other = count_ref[0]
    n_own = (total + IC - 1) // IC

    def sweep(span):
        def own_step(i, totals):
            first = pl.multiple_of(i * IC, IC)
            own = [mine_ref[axis, pl.ds(first, IC), :] for axis in range(3)]

            def other_block(first, sums):
                forces, totals = sums
                other = [near_ref[axis:axis + 1, pl.ds(first, 128)] for axis in range(3)]
                force, parts = pair_terms(own, other, span)
                forces = tuple(f + t for f, t in zip(forces, force))
                totals = tuple(t + ((p[0:8] + p[8:16]) + (p[16:24] + p[24:32])) for t, p in zip(totals, parts))
                return forces, totals

            def other_step(j, sums):
                first = pl.multiple_of(j * 256, 256)
                return other_block(first + 128, other_block(first, sums))

            def last_step(j, sums):
                return other_block(pl.multiple_of(n_other * 128 - 128, 128), sums)

            zero = jnp.zeros((IC, 128), jnp.float32)
            sums = lax.fori_loop(0, n_other // 2, other_step, ((zero,) * 3, totals))
            forces, totals = lax.fori_loop(0, n_other % 2, last_step, sums)
            for axis in range(3):
                acc_ref[axis, pl.ds(first, IC), :] = forces[axis]
            return totals

        zero = jnp.zeros((8, 128), jnp.float32)
        well, distance, pairs = lax.fori_loop(0, n_own, own_step, (zero,) * 3)
        energy = 2.0 * well - (0.5 * UPC) * distance - (0.5 * (UCUT - RC * UPC)) * pairs
        en_ref[...] = jnp.sum(energy, axis=0, keepdims=True)

    one_image = side[0, 0] >= 2.0 * RC

    @pl.when(one_image)
    def _():
        sweep(None)

    @pl.when(jnp.logical_not(one_image))
    def _():
        sweep(box)


def energy_kernel(en_ref, acc_ref, rows_ref, sum_ref, pos_ref, vel_ref, frc_ref, id_ref, ok_ref, force_ref, parts_ref, send_sem, recv_sem):
    barrier = greet()
    for axis in range(3):
        for b in range(PAD // 128):
            block = slice(128 * b, 128 * b + 128)
            force_ref[axis:axis + 1, block] = jnp.sum(jnp.transpose(acc_ref[axis, block, :]), axis=0, keepdims=True)
    pl.semaphore_wait(barrier, 7)
    copies = []
    for relation in FAR_FIRST:
        copy = pltpu.make_async_remote_copy(src_ref=en_ref, dst_ref=parts_ref.at[relation], send_sem=send_sem.at[relation], recv_sem=recv_sem.at[relation], device_id=partner(relation), device_id_type=MESH_ID)
        copy.start()
        copies.append(copy)
    rows = rows_ref[...]
    filled = rows[6:7, :] > 0.5
    force = jnp.where(filled, 24.0 * force_ref[...], 0.0)
    frc_ref[...] = force[:, 0:CAP]
    pos_ref[...] = rows[0:3, 0:CAP]
    vel_ref[...] = (rows[3:6, :] + (0.5 * DT) * force)[:, 0:CAP]
    new_id = (rows[6:7, :].astype(jnp.int32) - 1) * 65536 + rows[7:8, :].astype(jnp.int32)
    id_ref[...] = jnp.where(filled, new_id, 0)[:, 0:CAP].reshape(CAP)
    ok_ref[...] = filled.astype(jnp.int32)[:, 0:CAP].reshape(CAP)
    for copy in copies:
        copy.wait()
    parts_ref[0] = en_ref[...]
    over_x = [parts_ref[k] + parts_ref[k + 1] for k in (0, 2, 4, 6)]
    sum_ref[...] = (over_x[0] + over_x[1]) + (over_x[2] + over_x[3])


def store_kernel(sum_ref, *refs):
    sources, targets, total_ref, store_sem = refs[0:5], refs[5:11], refs[11], refs[12]
    stores = [pltpu.make_async_copy(sources[k], targets[k], store_sem.at[k]) for k in range(5)]
    for store in stores:
        store.start()
    total_ref[...] = jnp.sum(sum_ref[...], axis=1, keepdims=True)
    stores.append(pltpu.make_async_copy(total_ref, targets[5], store_sem.at[5]))
    stores[5].start()
    for store in stores:
        store.wait()


def solution(mesh):
    vmem = pl.BlockSpec(memory_space=pltpu.VMEM)
    hbm = pl.BlockSpec(memory_space=pltpu.HBM)
    f32, i32 = jnp.float32, jnp.int32

    def shape(dims, dtype=f32):
        return jax.ShapeDtypeStruct(dims, dtype)

    exchange = pl.pallas_call(
        exchange_kernel,
        out_shape=(shape((10, PAD)), shape((8, 1, 3 * PAD)), shape((8, 8, MIG))),
        in_specs=[hbm] * 5 + [pl.BlockSpec(memory_space=pl.ANY)],
        out_specs=(vmem, vmem, vmem),
        scratch_shapes=[pltpu.VMEM((3, CAP), f32)] * 3 + [pltpu.VMEM((CAP,), i32)] * 2 + [pltpu.VMEM((1, 1), f32), pltpu.VMEM((9, PAD), f32), pltpu.SemaphoreType.DMA((6,)), pltpu.SemaphoreType.DMA((2, 8)), pltpu.SemaphoreType.DMA((2, 8))],
        compiler_params=pltpu.CompilerParams(collective_id=0, has_side_effects=True, vmem_limit_bytes=16 << 20),
        name="exchange",
    )
    forces = pl.pallas_call(
        force_kernel,
        out_shape=(shape((1, 128)), shape((3, PAD, 128)), shape((8, PAD))),
        in_specs=[vmem] * 3,
        out_specs=(vmem,) * 3,
        scratch_shapes=[pltpu.VMEM((8, FULL), f32), pltpu.VMEM((8, 9 * PAD + 256), f32), pltpu.VMEM((3, PAD, 128), f32), pltpu.VMEM((3, 8, PAD), f32), pltpu.VMEM((8, 8, PAD + 128), f32), pltpu.VMEM((1, FULL), f32), pltpu.SMEM((1,), i32)],
        compiler_params=pltpu.CompilerParams(vmem_limit_bytes=16 << 20),
        name="forces",
    )
    results = (shape((3, CAP)), shape((3, CAP)), shape((3, CAP)), shape((CAP,), i32), shape((CAP,), i32))
    total_energy = pl.pallas_call(
        energy_kernel,
        out_shape=(shape((1, 128)),) + results,
        in_specs=[vmem] * 3,
        out_specs=(vmem,) * 6,
        scratch_shapes=[pltpu.VMEM((3, PAD), f32), pltpu.VMEM((8, 1, 128), f32), pltpu.SemaphoreType.DMA((8,)), pltpu.SemaphoreType.DMA((8,))],
        compiler_params=pltpu.CompilerParams(collective_id=1, has_side_effects=True, vmem_limit_bytes=16 << 20),
        name="energy",
    )
    store = pl.pallas_call(
        store_kernel,
        out_shape=results + (shape((1, 1)),),
        in_specs=[vmem] * 6,
        out_specs=(hbm,) * 6,
        scratch_shapes=[pltpu.VMEM((1, 1), f32), pltpu.SemaphoreType.DMA((6,))],
        compiler_params=pltpu.CompilerParams(vmem_limit_bytes=16 << 20),
        name="store",
    )

    def local_step(atom_pos, atom_vel, atom_frc, atom_id, atom_ok, brick_side):
        arrays = (atom_pos.T, atom_vel.T, atom_frc.T, atom_id, atom_ok, brick_side.reshape(1, 1))
        own, everyone, movers = exchange(*[pltpu.with_memory_space_constraint(array, pltpu.HBM) for array in arrays[:5]], arrays[5])
        partial, sums, rows = forces(own, everyone, movers)
        pos, vel, frc, new_id, new_ok, energy = store(*total_energy(partial, sums, rows))
        return pos.T, vel.T, frc.T, new_id, new_ok, energy.reshape(())

    row_spec = P(MESH_AXES, None)
    id_spec = P(MESH_AXES)
    return jax.shard_map(local_step, mesh=mesh, in_specs=(row_spec, row_spec, row_spec, id_spec, id_spec, P()), out_specs=(row_spec, row_spec, row_spec, id_spec, id_spec, P()), check_vma=False)
```

profile of v0, /device:TPU:0, one launch (start us, length us, event | category | flops | bytes accessed | tf_op | source)
XLA Modules:
  0.0 20.1 jit_solution(3594585154239845465)
XLA Ops:
  1.3 7.6 %exchange.1 = (f32[10,768]{1,0:T(8,128)S(1)}, f32[8,1,2304]{2,1,0:T(1,128)S(1)}, f32[8,8,256]{2,1,0:T(8,128)S(1)}) custom-call(f32[3,729]{1,0:T(4,128)} %bitcast.9, f32[3,729]{1,0:T(4,128)} %bitcast.10, f32[3,729]{1,0:T(4,128)} %bitcast.11, s32[729]{0:T(1024)} %id_hbm.1, s32[729]{0:T(1024)} %ok_hbm.1, f32[1,1]{1,0:T(1,128)} %bitcast.8.side_hbm), custom_call_target="tpu_custom_call" | custom-call | tf_op jit(solution)/shard_map/exchange/pallas_call | solution.py:390
  8.9 5.6 %forces.1 = (f32[1,128]{1,0:T(1,128)S(1)}, f32[3,768,128]{2,1,0:T(8,128)S(1)}, f32[8,768]{1,0:T(8,128)S(1)}) custom-call(f32[10,768]{1,0:T(8,128)S(1)} %get-tuple-element.24.own_ref, f32[8,1,2304]{2,1,0:T(1,128)S(1)} %get-tuple-element.25.all_ref, f32[8,8,256]{2,1,0:T(8,128)S(1)} %get-tuple-element.26.mig_ref), custom_call_target="tpu_custom_call" | custom-call | tf_op jit(solution)/shard_map/forces/pallas_call | solution.py:391
  14.5 4.9 %energy.1 = (f32[1,128]{1,0:T(1,128)S(1)}, f32[3,729]{1,0:T(4,128)S(1)}, f32[3,729]{1,0:T(4,128)S(1)}, f32[3,729]{1,0:T(4,128)S(1)}, s32[729]{0:T(1024)S(1)}, /*index=5*/s32[729]{0:T(1024)S(1)}) custom-call(f32[1,128]{1,0:T(1,128)S(1)} %get-tuple-element.27.en_ref, f32[3,768,128]{2,1,0:T(8,128)S(1)} %get-tuple-element.28.acc_ref, ...), custom_call_target="tpu_custom_call" | custom-call | tf_op jit(solution)/shard_map/energy/pallas_call | solution.py:392
  19.4 0.7 %store.1 = (f32[3,729]{1,0:T(4,128)}, f32[3,729]{1,0:T(4,128)}, f32[3,729]{1,0:T(4,128)}, s32[729]{0:T(1024)}, s32[729]{0:T(1024)}, /*index=5*/f32[1,1]{1,0:T(1,128)}) custom-call(f32[1,128]{1,0:T(1,128)S(1)} %get-tuple-element.30.sum_ref, f32[3,729]{1,0:T(4,128)S(1)} %get-tuple-element.31.refs_0_, f32[3,729]{1,0:T(4,128)S(1)} %get-tuple-element.32.refs_1_, ...), custom_call_target="tpu_custom_call" | custom-call | tf_op jit(solution)/shard_map/store/pallas_call | solution.py:392
where the time goes:
time: 20.3 us; the launch traced here: 20.1 us
  Pallas kernels  18.8 us (93%)
  between operations  1.3 us (6%)
    pallas_call x1, Pallas kernels, local_step(): exchange(*[pltpu.with_memory_space_constraint(array, pltpu.HBM) for array...  7.61 us
    pallas_call x1, Pallas kernels, local_step(): partial, sums, rows = forces(own, everyone, movers)  5.58 us
    pallas_call x1, Pallas kernels, local_step(): total_energy(partial, sums, rows)  4.93 us
    pallas_call x1, Pallas kernels, local_step(): store(*total_energy(partial, sums, rows))  0.67 us

commit v1 on v0

v1 whole, which is shorter than its diff:
```python
import functools

import jax
import jax.numpy as jnp
from jax import lax
from jax.experimental import pallas as pl
from jax.experimental.pallas import tpu as pltpu
from jax.sharding import PartitionSpec as P

DT = 0.005
RC = 2.5
FAR_AWAY = 1.0e6
UCUT = 4.0 * (RC ** -12 - RC ** -6)
UPC = -48.0 * RC ** -13 + 24.0 * RC ** -7
MESH_AXES = ("z", "y", "x")
CAP = 729
PAD = 768
MIG = 256
SEG = {1: (0, 16), 2: (16, 16), 4: (32, 16), 3: (48, 32), 5: (80, 32), 6: (128, 32), 7: (160, 64)}
IC = 32
NARROW = 512
LANES = 128
ID_SPLIT = 65536
NT = (((1,), (1,)), ((), ()))
OTHERS = tuple(range(1, 8))
FAR_FIRST = (6, 7, 4, 2, 5, 3, 1)
REACH = RC + 0.01
MESH_ID = pl.DeviceIdType.MESH


def pieces_of(rows):
    first = rows.astype(jnp.bfloat16).astype(jnp.float32)
    rest = rows - first
    second = rest.astype(jnp.bfloat16).astype(jnp.float32)
    third = rest - second
    return jnp.concatenate([first, second, third], axis=0).astype(jnp.bfloat16)


def select_rows(rows, onehot):
    out = lax.dot_general(pieces_of(rows), onehot, NT, preferred_element_type=jnp.float32)
    return sum_groups(out, rows.shape[0])


def sum_groups(rows, size):
    total = rows[0:size]
    for k in range(size, rows.shape[0], size):
        total = total + rows[k:k + size]
    return total


def as_bf16(mask):
    return mask.astype(jnp.float32).astype(jnp.bfloat16)


def iota(dims, axis, dtype=jnp.float32):
    return lax.broadcasted_iota(jnp.int32, dims, axis).astype(dtype)


def id_of(rows):
    return (rows[6:7].astype(jnp.int32) - 1) * ID_SPLIT + rows[7:8].astype(jnp.int32)


def partner(relation):
    return tuple((lax.axis_index(name) + relation // bit) % 2 for name, bit in zip(MESH_AXES, (4, 2, 1)))


def greet():
    barrier = pltpu.get_barrier_semaphore()
    for relation in OTHERS:
        pl.semaphore_signal(barrier, inc=1, device_id=partner(relation), device_id_type=MESH_ID)
    return barrier


def send_all(pairs, send_sem, recv_sem):
    copies = []
    for relation in FAR_FIRST:
        for which, (src, dst) in enumerate(pairs(relation)):
            copy = pltpu.make_async_remote_copy(src_ref=src, dst_ref=dst, send_sem=send_sem.at[which, relation], recv_sem=recv_sem.at[which, relation], device_id=partner(relation), device_id_type=MESH_ID)
            copy.start()
            copies.append(copy)
    return copies


def axis_column(values, rows):
    idx = lax.broadcasted_iota(jnp.int32, (rows, 1), 0)
    out = jnp.full((rows, 1), values[-1], jnp.float32)
    for k in range(len(values) - 1):
        out = jnp.where(idx == k, values[k], out)
    return out


def brick_coords():
    return [lax.axis_index(name).astype(jnp.float32) for name in ("x", "y", "z")]


def prefix_counts(member):
    member = member.astype(jnp.float32)
    starts = range(0, member.shape[1], LANES)
    stacked = as_bf16(jnp.concatenate([member[:, k:k + LANES] for k in starts], axis=0) > 0.5)
    col = iota((LANES, 2 * LANES), 1)
    ladder = as_bf16((iota((LANES, 2 * LANES), 0) < col) | (col >= LANES))
    counts = jnp.dot(stacked, ladder, preferred_element_type=jnp.float32)
    before = jnp.zeros((8, LANES), jnp.float32)
    ranks = []
    for k in range(0, counts.shape[0], 8):
        ranks.append(counts[k:k + 8, 0:LANES] + before)
        before = before + counts[k:k + 8, LANES:]
    return jnp.concatenate(ranks, axis=1), before


def exchange_kernel(pos_hbm, vel_hbm, frc_hbm, id_hbm, ok_hbm, side_hbm, own_ref, all_ref, mig_ref, pos_ref, vel_ref, frc_ref, id_ref, ok_ref, side_ref, pad_ref, load_sem, send_sem, recv_sem):
    loads = []
    for k, (src, dst) in enumerate(((pos_hbm, pos_ref), (vel_hbm, vel_ref), (frc_hbm, frc_ref), (id_hbm, id_ref), (ok_hbm, ok_ref), (side_hbm, side_ref))):
        load = pltpu.make_async_copy(src, dst, load_sem.at[k])
        load.start()
        loads.append(load)
    barrier = greet()
    pad_ref[...] = jnp.zeros_like(pad_ref)
    for load in loads:
        load.wait()
    side = side_ref[...]
    box = side * 2.0
    half_v = vel_ref[...] + (0.5 * DT) * frc_ref[...]
    pad_ref[0:3, 0:CAP] = pos_ref[...] + DT * half_v
    pad_ref[3:6, 0:CAP] = half_v
    pad_ref[6:7, 0:CAP] = (id_ref[...].reshape(1, CAP) // ID_SPLIT).astype(jnp.float32) + 1.0
    pad_ref[7:8, 0:CAP] = (id_ref[...].reshape(1, CAP) % ID_SPLIT).astype(jnp.float32)
    pad_ref[8:9, 0:CAP] = ok_ref[...].reshape(1, CAP).astype(jnp.float32)
    unwrapped = pad_ref[0:3, :]
    owned = pad_ref[8:9, :] > 0.5
    moved = jnp.where(unwrapped < 0.0, unwrapped + box, jnp.where(unwrapped >= box, unwrapped - box, unwrapped))
    for axis in range(3):
        all_ref[0, :, PAD * axis:PAD * (axis + 1)] = jnp.where(owned, moved[axis:axis + 1, :], FAR_AWAY)

    low = axis_column([coord * side for coord in brick_coords()], 3)
    outside = (unwrapped < low) | (unwrapped >= low + side)
    bits = jnp.where(outside, axis_column([1.0, 2.0, 4.0], 3), 0.0)
    code = jnp.sum(bits, axis=0, keepdims=True)
    code = jnp.where(owned, code, -1.0)
    member = code == iota((8, PAD), 0)
    rank, _ = prefix_counts(member)
    offset = axis_column([0.0] + [float(SEG[m][0]) for m in OTHERS], 8)
    slot = jnp.sum(jnp.where(member, rank + offset, 0.0), axis=0, keepdims=True)
    rows = jnp.concatenate([moved, pad_ref[3:8, :]], axis=0)
    mig_ref[0] = select_rows(rows, as_bf16(iota((MIG, PAD), 0) == jnp.where(code > 0.5, slot, -1.0)))
    own_ref[8:9, :] = jnp.broadcast_to(side, (1, PAD))

    def pairs(relation):
        block = pl.ds(SEG[relation][0] // LANES * LANES, LANES)
        return (mig_ref.at[0, :, block], mig_ref.at[relation, :, block]), (all_ref.at[0], all_ref.at[relation])

    pl.semaphore_wait(barrier, len(OTHERS))
    copies = send_all(pairs, send_sem, recv_sem)
    pieces = pieces_of(rows)
    slots = iota((LANES, PAD), 0)
    slot = jnp.where(code == 0.0, slot, -1.0)

    def pack(k, carry):
        first = k * LANES
        out = lax.dot_general(pieces, as_bf16(slots == slot - first.astype(jnp.float32)), NT, preferred_element_type=jnp.float32)
        own_ref[0:8, pl.ds(pl.multiple_of(first, LANES), LANES)] = sum_groups(out, 8)
        return carry

    lax.fori_loop(0, PAD // LANES, pack, 0)
    for copy in copies:
        copy.wait()


def pair_terms(own, other, span):
    delta = []
    for mine, theirs in zip(own, other):
        diff = mine - theirs
        if span is not None:
            diff = diff - jnp.where(diff > 0.5 * span, span, jnp.where(diff < -0.5 * span, -span, 0.0))
        delta.append(diff)
    dist_sq = delta[0] * delta[0] + delta[1] * delta[1] + delta[2] * delta[2]
    in_range = (dist_sq < RC * RC) & (dist_sq > 0.01)
    inv_r = jnp.where(in_range, lax.rsqrt(dist_sq), 0.0)
    inv_r2 = inv_r * inv_r
    inv_r6 = inv_r2 * inv_r2 * inv_r2
    inv_r12 = inv_r6 * inv_r6
    well = inv_r12 - inv_r6
    scale = (well + inv_r12) * inv_r2 + (UPC / 24.0) * inv_r
    return [scale * d for d in delta], [well, dist_sq * inv_r, jnp.where(in_range, 1.0, 0.0)]


def force_kernel(own_ref, all_ref, mig_ref, en_ref, acc_ref, rows_ref, near_ref, mine_ref, plane_ref, list_ref, count_ref):
    side = own_ref[8:9, 0:1]
    box = side * 2.0
    lane = iota((1, MIG), 1, jnp.int32)
    arrivals = jnp.zeros((8, MIG), jnp.float32)
    for relation, (start, size) in SEG.items():
        arrivals = jnp.where((lane >= start) & (lane < start + size), mig_ref[relation], arrivals)
    arrived = arrivals[6:7, :] > 0.5
    staying = (own_ref[6:7, :] > 0.5).astype(jnp.float32)
    n_staying = jnp.sum(staying, axis=1, keepdims=True)
    total = jnp.sum((n_staying + jnp.sum(arrived.astype(jnp.float32), axis=1, keepdims=True)).astype(jnp.int32))
    tail = all_ref[0, :, NARROW:PAD]
    for relation in OTHERS:
        tail = jnp.minimum(tail, all_ref[relation, :, NARROW:PAD])
    narrow = (jnp.min(tail) > 0.5 * FAR_AWAY) & (total <= NARROW)
    slot, _ = prefix_counts(jnp.broadcast_to(arrived, (8, MIG)))
    slot = jnp.where(arrived, slot[0:1, :] + n_staying, -1.0)
    pieces = pieces_of(arrivals)
    centre = [(coord + 0.5) * side for coord in brick_coords()]

    def prepare(width):
        for relation in range(8):
            for axis in range(3):
                plane_ref[axis, relation:relation + 1, 0:width] = all_ref[relation, :, PAD * axis:PAD * axis + width]
        planes = []
        beyond = jnp.zeros((8, width), jnp.float32)
        for axis in range(3):
            theirs = plane_ref[axis, :, 0:width] - centre[axis]
            theirs = jnp.where(theirs > side, theirs - box, jnp.where(theirs < -side, theirs + box, theirs))
            excess = jnp.maximum(jnp.abs(theirs) - 0.5 * side, 0.0)
            beyond = beyond + excess * excess
            planes.append(theirs)
        keep = (beyond < REACH * REACH) & (beyond > 0.0)
        front, held = prefix_counts(keep)
        lanes = iota((8, width), 1, jnp.int32)
        hops = jnp.where(keep, lanes - front.astype(jnp.int32), 0)

        slots = iota((LANES, MIG), 0)
        done = 0
        for bit in range(10 if width > 512 else 9):
            step = 1 << bit
            coming = pltpu.roll(hops, width - step, 1)
            take = (coming & step) != 0
            leave = (hops & step) != 0
            hops = jnp.where(take, coming, jnp.where(leave, 0, hops))
            planes = [jnp.where(take, pltpu.roll(plane, width - step, 1), plane) for plane in planes]
            if done < width:
                out = lax.dot_general(pieces, as_bf16(slots == slot - float(done)), NT, preferred_element_type=jnp.float32)
                rows_ref[:, done:done + LANES] = own_ref[0:8, done:done + LANES] + sum_groups(out, 8)
                done += LANES
        if width < PAD:
            rows_ref[:, width:PAD] = jnp.zeros((8, PAD - width), jnp.float32)

        rows = rows_ref[:, 0:width]
        filled = rows[6:7, :] > 0.5
        local = rows[0:3, :] - axis_column(centre, 3)
        near_ref[0:3, 0:width] = jnp.where(filled, local, FAR_AWAY)
        local = jnp.concatenate([jnp.where(filled, local, -FAR_AWAY), jnp.zeros((5, width), jnp.float32)], axis=0)
        spread = as_bf16(iota((24, 3 * LANES), 0, jnp.int32) % 8 == iota((24, 3 * LANES), 1, jnp.int32) // LANES)
        columns = lax.dot_general(pieces_of(local), spread, (((0,), (0,)), ((), ())), preferred_element_type=jnp.float32)
        for axis in range(3):
            mine_ref[axis, 0:width, :] = columns[:, LANES * axis:LANES * (axis + 1)]

        for relation in range(8):
            for axis in range(3):
                list_ref[relation, axis:axis + 1, 0:width] = planes[axis][relation:relation + 1, :]
        held = held.astype(jnp.int32)
        lane128 = iota((8, LANES), 1, jnp.int32)
        start = total
        for relation in range(8):
            into = start % LANES
            first = pl.multiple_of(start - into, LANES)
            turned = pltpu.roll(list_ref[relation, :, 0:width + LANES], into, 1)
            near_ref[:, pl.ds(first, LANES)] = jnp.where(lane128 < into, near_ref[:, pl.ds(first, LANES)], turned[:, 0:LANES])
            near_ref[:, pl.ds(pl.multiple_of(first + LANES, LANES), width)] = turned[:, LANES:]
            start = start + held[relation, 0]
        into = start % LANES
        first = pl.multiple_of(start - into, LANES)
        near_ref[:, pl.ds(first, LANES)] = jnp.where(lane128 < into, near_ref[:, pl.ds(first, LANES)], FAR_AWAY)
        count_ref[0] = (start + LANES - 1) // LANES

    @pl.when(narrow)
    def _():
        prepare(NARROW)

    @pl.when(jnp.logical_not(narrow))
    def _():
        prepare(PAD)

    n_other = count_ref[0]
    n_own = (total + IC - 1) // IC

    def sweep(span):
        def own_step(i, totals):
            first = pl.multiple_of(i * IC, IC)
            own = [mine_ref[axis, pl.ds(first, IC), :] for axis in range(3)]

            def other_block(first, sums):
                forces, totals = sums
                other = [near_ref[axis:axis + 1, pl.ds(first, LANES)] for axis in range(3)]
                force, parts = pair_terms(own, other, span)
                forces = tuple(f + t for f, t in zip(forces, force))
                totals = tuple(t + sum_groups(p, 8) for t, p in zip(totals, parts))
                return forces, totals

            def other_step(j, sums):
                first = pl.multiple_of(j * 2 * LANES, 2 * LANES)
                return other_block(first + LANES, other_block(first, sums))

            def last_step(j, sums):
                return other_block(pl.multiple_of((n_other - 1) * LANES, LANES), sums)

            zero = jnp.zeros((IC, LANES), jnp.float32)
            sums = lax.fori_loop(0, n_other // 2, other_step, ((zero,) * 3, totals))
            forces, totals = lax.fori_loop(0, n_other % 2, last_step, sums)
            for axis in range(3):
                acc_ref[axis, pl.ds(first, IC), :] = forces[axis]
            return totals

        zero = jnp.zeros((8, LANES), jnp.float32)
        well, distance, pairs = lax.fori_loop(0, n_own, own_step, (zero,) * 3)
        energy = 2.0 * well - (0.5 * UPC) * distance - (0.5 * (UCUT - RC * UPC)) * pairs
        en_ref[...] = jnp.sum(energy, axis=0, keepdims=True)

    one_image = side[0, 0] >= 2.0 * RC

    @pl.when(one_image)
    def _():
        sweep(None)

    @pl.when(jnp.logical_not(one_image))
    def _():
        sweep(box)


def energy_kernel(en_ref, acc_ref, rows_ref, sum_ref, pos_ref, vel_ref, frc_ref, id_ref, ok_ref, force_ref, parts_ref, send_sem, recv_sem):
    barrier = greet()
    pl.semaphore_wait(barrier, len(OTHERS))
    copies = send_all(lambda relation: ((en_ref, parts_ref.at[relation]),), send_sem, recv_sem)
    def turn(k, carry):
        block = pl.ds(pl.multiple_of(k * LANES, LANES), LANES)
        for axis in range(3):
            force_ref[axis:axis + 1, block] = jnp.sum(jnp.transpose(acc_ref[axis, block, :]), axis=0, keepdims=True)
        return carry

    lax.fori_loop(0, PAD // LANES, turn, 0)
    rows = rows_ref[...]
    filled = rows[6:7, :] > 0.5
    key = jnp.where(filled, id_of(rows), 2147483647)
    key_col = jnp.transpose(jnp.broadcast_to(key, (8, PAD)))[:, 0:1]
    slot = jnp.dot(jnp.ones((8, PAD), jnp.bfloat16), as_bf16(key_col < key), preferred_element_type=jnp.float32)[0:1, :]
    onehot = as_bf16(iota((PAD, PAD), 0) == jnp.where(filled, slot, -1.0))
    force_ref[0:3, :] = jnp.where(filled, (24.0 * force_ref[0:3, :]), 0.0)
    force_ref[3:8, :] = jnp.zeros((5, PAD), jnp.float32)
    out = select_rows(jnp.concatenate([rows, force_ref[...]], axis=0), onehot)[:, 0:CAP]
    force = out[8:11]
    filled = out[6:7] > 0.5
    frc_ref[...] = force
    pos_ref[...] = out[0:3]
    vel_ref[...] = out[3:6] + (0.5 * DT) * force
    id_ref[...] = jnp.where(filled, id_of(out), 0).reshape(CAP)
    ok_ref[...] = filled.astype(jnp.int32).reshape(CAP)
    for copy in copies:
        copy.wait()
    parts_ref[0] = en_ref[...]
    level = [parts_ref[relation] for relation in range(8)]
    while len(level) > 1:
        level = [one + two for one, two in zip(level[0::2], level[1::2])]
    sum_ref[...] = level[0]


def store_kernel(sum_ref, *refs):
    sources, targets, total_ref, store_sem = refs[0:5], refs[5:11], refs[11], refs[12]
    stores = [pltpu.make_async_copy(sources[k], targets[k], store_sem.at[k]) for k in range(5)]
    for store in stores:
        store.start()
    total_ref[...] = jnp.sum(sum_ref[...], axis=1, keepdims=True)
    stores.append(pltpu.make_async_copy(total_ref, targets[5], store_sem.at[5]))
    stores[5].start()
    for store in stores:
        store.wait()


def solution(mesh):
    vmem = pl.BlockSpec(memory_space=pltpu.VMEM)
    hbm = pl.BlockSpec(memory_space=pltpu.HBM)
    f32, i32 = jnp.float32, jnp.int32

    def shape(dims, dtype=f32):
        return jax.ShapeDtypeStruct(dims, dtype)

    exchange = pl.pallas_call(
        exchange_kernel,
        out_shape=(shape((9, PAD)), shape((8, 1, 3 * PAD)), shape((8, 8, MIG))),
        in_specs=[hbm] * 5 + [pl.BlockSpec(memory_space=pl.ANY)],
        out_specs=(vmem, vmem, vmem),
        scratch_shapes=[pltpu.VMEM((3, CAP), f32)] * 3 + [pltpu.VMEM((CAP,), i32)] * 2 + [pltpu.VMEM((1, 1), f32), pltpu.VMEM((9, PAD), f32), pltpu.SemaphoreType.DMA((6,)), pltpu.SemaphoreType.DMA((2, 8)), pltpu.SemaphoreType.DMA((2, 8))],
        compiler_params=pltpu.CompilerParams(collective_id=0, has_side_effects=True, vmem_limit_bytes=16 << 20),
        name="exchange",
    )
    forces = pl.pallas_call(
        force_kernel,
        out_shape=(shape((1, 128)), shape((3, PAD, 128)), shape((8, PAD))),
        in_specs=[vmem] * 3,
        out_specs=(vmem,) * 3,
        scratch_shapes=[pltpu.VMEM((8, 9 * PAD + 256), f32), pltpu.VMEM((3, PAD, 128), f32), pltpu.VMEM((3, 8, PAD), f32), pltpu.VMEM((8, 8, PAD + 128), f32), pltpu.SMEM((1,), i32)],
        compiler_params=pltpu.CompilerParams(vmem_limit_bytes=16 << 20),
        name="forces",
    )
    results = (shape((3, CAP)), shape((3, CAP)), shape((3, CAP)), shape((CAP,), i32), shape((CAP,), i32))
    total_energy = pl.pallas_call(
        energy_kernel,
        out_shape=(shape((1, 128)),) + results,
        in_specs=[vmem] * 3,
        out_specs=(vmem,) * 6,
        scratch_shapes=[pltpu.VMEM((8, PAD), f32), pltpu.VMEM((8, 1, LANES), f32), pltpu.SemaphoreType.DMA((1, 8)), pltpu.SemaphoreType.DMA((1, 8))],
        compiler_params=pltpu.CompilerParams(collective_id=1, has_side_effects=True, vmem_limit_bytes=16 << 20),
        name="energy",
    )
    store = pl.pallas_call(
        store_kernel,
        out_shape=results + (shape((1, 1)),),
        in_specs=[vmem] * 6,
        out_specs=(hbm,) * 6,
        scratch_shapes=[pltpu.VMEM((1, 1), f32), pltpu.SemaphoreType.DMA((6,))],
        compiler_params=pltpu.CompilerParams(vmem_limit_bytes=16 << 20),
        name="store",
    )

    def local_step(atom_pos, atom_vel, atom_frc, atom_id, atom_ok, brick_side):
        arrays = (atom_pos.T, atom_vel.T, atom_frc.T, atom_id, atom_ok, brick_side.reshape(1, 1))
        own, everyone, movers = exchange(*[pltpu.with_memory_space_constraint(array, pltpu.HBM) for array in arrays[:5]], arrays[5])
        partial, sums, rows = forces(own, everyone, movers)
        pos, vel, frc, new_id, new_ok, energy = store(*total_energy(partial, sums, rows))
        return pos.T, vel.T, frc.T, new_id, new_ok, energy.reshape(())

    row_spec = P(MESH_AXES, None)
    id_spec = P(MESH_AXES)
    return jax.shard_map(local_step, mesh=mesh, in_specs=(row_spec, row_spec, row_spec, id_spec, id_spec, P()), out_specs=(row_spec, row_spec, row_spec, id_spec, id_spec, P()), check_vma=False)
```

time: 20.3 us -> 19.5 us (0.961)
  Pallas kernels: 18.8 us -> 17.9 us
    pallas_call x1, Pallas kernels: 5.58 us -> 4.86 us  [local_step(): partial, sums, rows = forces(own, everyone, movers)]
    pallas_call x1, Pallas kernels: 4.93 us -> 4.72 us  [local_step(): total_energy(partial, sums, rows)]
where the time goes in v1:
time: 19.5 us; the launch traced here: 19.2 us
  Pallas kernels  17.9 us (92%)
  between operations  1.3 us (7%)
    pallas_call x1, Pallas kernels, local_step(): exchange(*[pltpu.with_memory_space_constraint(array, pltpu.HBM) for array...  7.61 us
    pallas_call x1, Pallas kernels, local_step(): partial, sums, rows = forces(own, everyone, movers)  4.86 us
    pallas_call x1, Pallas kernels, local_step(): total_energy(partial, sums, rows)  4.72 us
    pallas_call x1, Pallas kernels, local_step(): store(*total_energy(partial, sums, rows))  0.67 us

profile of v1, /device:TPU:0, one launch (start us, length us, event | category | flops | bytes accessed | tf_op | source)
XLA Modules:
  0.0 19.2 jit_solution(13389655180100559544)
XLA Ops:
  1.3 7.6 %exchange.1 = (f32[9,768]{1,0:T(8,128)S(1)}, f32[8,1,2304]{2,1,0:T(1,128)S(1)}, f32[8,8,256]{2,1,0:T(8,128)S(1)}) custom-call(f32[3,729]{1,0:T(4,128)} %bitcast.9, f32[3,729]{1,0:T(4,128)} %bitcast.10, f32[3,729]{1,0:T(4,128)} %bitcast.11, s32[729]{0:T(1024)} %id_hbm.1, s32[729]{0:T(1024)} %ok_hbm.1, f32[1,1]{1,0:T(1,128)} %bitcast.8.side_hbm), custom_call_target="tpu_custom_call" | custom-call | tf_op jit(solution)/shard_map/exchange/pallas_call | solution.py:418
  8.9 4.9 %forces.1 = (f32[1,128]{1,0:T(1,128)S(1)}, f32[3,768,128]{2,1,0:T(8,128)S(1)}, f32[8,768]{1,0:T(8,128)S(1)}) custom-call(f32[9,768]{1,0:T(8,128)S(1)} %get-tuple-element.24.own_ref, f32[8,1,2304]{2,1,0:T(1,128)S(1)} %get-tuple-element.25.all_ref, f32[8,8,256]{2,1,0:T(8,128)S(1)} %get-tuple-element.26.mig_ref), custom_call_target="tpu_custom_call" | custom-call | tf_op jit(solution)/shard_map/forces/pallas_call | solution.py:419
  13.8 4.7 %energy.1 = (f32[1,128]{1,0:T(1,128)S(1)}, f32[3,729]{1,0:T(4,128)S(1)}, f32[3,729]{1,0:T(4,128)S(1)}, f32[3,729]{1,0:T(4,128)S(1)}, s32[729]{0:T(1024)S(1)}, /*index=5*/s32[729]{0:T(1024)S(1)}) custom-call(f32[1,128]{1,0:T(1,128)S(1)} %get-tuple-element.27.en_ref, f32[3,768,128]{2,1,0:T(8,128)S(1)} %get-tuple-element.28.acc_ref, ...), custom_call_target="tpu_custom_call" | custom-call | tf_op jit(solution)/shard_map/energy/pallas_call | solution.py:420
  18.5 0.7 %store.1 = (f32[3,729]{1,0:T(4,128)}, f32[3,729]{1,0:T(4,128)}, f32[3,729]{1,0:T(4,128)}, s32[729]{0:T(1024)}, s32[729]{0:T(1024)}, /*index=5*/f32[1,1]{1,0:T(1,128)}) custom-call(f32[1,128]{1,0:T(1,128)S(1)} %get-tuple-element.30.sum_ref, f32[3,729]{1,0:T(4,128)S(1)} %get-tuple-element.31.refs_0_, f32[3,729]{1,0:T(4,128)S(1)} %get-tuple-element.32.refs_1_, ...), custom_call_target="tpu_custom_call" | custom-call | tf_op jit(solution)/shard_map/store/pallas_call | solution.py:420

commit v2 on v1

--- a/solution.py
+++ b/solution.py
@@ -66,7 +66,7 @@
 
 def greet():
     barrier = pltpu.get_barrier_semaphore()
-    for relation in OTHERS:
+    for relation in FAR_FIRST:
         pl.semaphore_signal(barrier, inc=1, device_id=partner(relation), device_id_type=MESH_ID)
     return barrier
 
@@ -137,13 +137,14 @@
     bits = jnp.where(outside, axis_column([1.0, 2.0, 4.0], 3), 0.0)
     code = jnp.sum(bits, axis=0, keepdims=True)
     code = jnp.where(owned, code, -1.0)
-    member = code == iota((8, PAD), 0)
+    lower = moved[2:3, :] < low[2:3, :] + 0.5 * side
+    member = jnp.where((code == 0.0) & jnp.logical_not(lower), -1.0, code) == iota((8, PAD), 0)
     rank, _ = prefix_counts(member)
     offset = axis_column([0.0] + [float(SEG[m][0]) for m in OTHERS], 8)
     slot = jnp.sum(jnp.where(member, rank + offset, 0.0), axis=0, keepdims=True)
     rows = jnp.concatenate([moved, pad_ref[3:8, :]], axis=0)
     mig_ref[0] = select_rows(rows, as_bf16(iota((MIG, PAD), 0) == jnp.where(code > 0.5, slot, -1.0)))
-    own_ref[8:9, :] = jnp.broadcast_to(side, (1, PAD))
+    own_ref[16:17, :] = jnp.broadcast_to(side, (1, PAD))
 
     def pairs(relation):
         block = pl.ds(SEG[relation][0] // LANES * LANES, LANES)
@@ -153,12 +154,14 @@
     copies = send_all(pairs, send_sem, recv_sem)
     pieces = pieces_of(rows)
     slots = iota((LANES, PAD), 0)
-    slot = jnp.where(code == 0.0, slot, -1.0)
+    upper_slot = iota((1, PAD), 1) - jnp.sum(rank, axis=0, keepdims=True)
+    halves = (jnp.where((code == 0.0) & lower, slot, -1.0), jnp.where((code == 0.0) & jnp.logical_not(lower), upper_slot, -1.0))
 
     def pack(k, carry):
         first = k * LANES
-        out = lax.dot_general(pieces, as_bf16(slots == slot - first.astype(jnp.float32)), NT, preferred_element_type=jnp.float32)
-        own_ref[0:8, pl.ds(pl.multiple_of(first, LANES), LANES)] = sum_groups(out, 8)
+        for half, target in enumerate(halves):
+            out = lax.dot_general(pieces, as_bf16(slots == target - first.astype(jnp.float32)), NT, preferred_element_type=jnp.float32)
+            own_ref[8 * half:8 * half + 8, pl.ds(pl.multiple_of(first, LANES), LANES)] = sum_groups(out, 8)
         return carry
 
     lax.fori_loop(0, PAD // LANES, pack, 0)
@@ -184,106 +187,130 @@
     return [scale * d for d in delta], [well, dist_sq * inv_r, jnp.where(in_range, 1.0, 0.0)]
 
 
-def force_kernel(own_ref, all_ref, mig_ref, en_ref, acc_ref, rows_ref, near_ref, mine_ref, plane_ref, list_ref, count_ref):
-    side = own_ref[8:9, 0:1]
+def force_kernel(own_ref, all_ref, mig_ref, en_ref, acc_ref, rows_ref, near_ref, mine_ref, plane_ref, list_ref, dense_ref, count_ref):
+    side = own_ref[16:17, 0:1]
     box = side * 2.0
+    centre = [(coord + 0.5) * side for coord in brick_coords()]
     lane = iota((1, MIG), 1, jnp.int32)
     arrivals = jnp.zeros((8, MIG), jnp.float32)
     for relation, (start, size) in SEG.items():
         arrivals = jnp.where((lane >= start) & (lane < start + size), mig_ref[relation], arrivals)
-    arrived = arrivals[6:7, :] > 0.5
-    staying = (own_ref[6:7, :] > 0.5).astype(jnp.float32)
-    n_staying = jnp.sum(staying, axis=1, keepdims=True)
-    total = jnp.sum((n_staying + jnp.sum(arrived.astype(jnp.float32), axis=1, keepdims=True)).astype(jnp.int32))
+    half_of = jnp.where(arrivals[2:3, :] < centre[2], 0.0, 1.0)
+    arrived = jnp.where(arrivals[6:7, :] > 0.5, half_of, -1.0) == iota((8, MIG), 0)
+    ranks, _ = prefix_counts(arrived)
+    targets, sizes = [], []
+    for half in range(2):
+        staying = jnp.sum((own_ref[8 * half + 6:8 * half + 7, :] > 0.5).astype(jnp.float32), axis=1, keepdims=True)
+        here = arrived[half:half + 1, :]
+        targets.append(jnp.where(here, ranks[half:half + 1, :] + staying, -1.0))
+        sizes.append(jnp.sum((staying + jnp.sum(here.astype(jnp.float32), axis=1, keepdims=True)).astype(jnp.int32)))
+    split = (sizes[0] + IC - 1) // IC * IC
+    total = split + sizes[1]
     tail = all_ref[0, :, NARROW:PAD]
     for relation in OTHERS:
         tail = jnp.minimum(tail, all_ref[relation, :, NARROW:PAD])
-    narrow = (jnp.min(tail) > 0.5 * FAR_AWAY) & (total <= NARROW)
-    slot, _ = prefix_counts(jnp.broadcast_to(arrived, (8, MIG)))
-    slot = jnp.where(arrived, slot[0:1, :] + n_staying, -1.0)
+    narrow = (jnp.min(tail) > 0.5 * FAR_AWAY) & (total <= NARROW + LANES) & (jnp.maximum(sizes[0], sizes[1]) <= NARROW - LANES)
     pieces = pieces_of(arrivals)
-    centre = [(coord + 0.5) * side for coord in brick_coords()]
-
-    def prepare(width):
+
+    def lay(target, rows, start):
+        into = start % LANES
+        first = pl.multiple_of(start - into, LANES)
+        turned = pltpu.roll(rows, into, 1)
+        behind = iota((8, LANES), 1, jnp.int32) >= into
+        pltpu.store(target.at[:, pl.ds(first, LANES)], turned[:, 0:LANES], mask=behind)
+        target[:, pl.ds(pl.multiple_of(first + LANES, LANES), rows.shape[1] - LANES)] = turned[:, LANES:]
+
+    def prepare(width, half_width, slots_width):
         for relation in range(8):
             for axis in range(3):
                 plane_ref[axis, relation:relation + 1, 0:width] = all_ref[relation, :, PAD * axis:PAD * axis + width]
-        planes = []
-        beyond = jnp.zeros((8, width), jnp.float32)
+        places = []
+        across = jnp.zeros((8, width), jnp.float32)
         for axis in range(3):
             theirs = plane_ref[axis, :, 0:width] - centre[axis]
             theirs = jnp.where(theirs > side, theirs - box, jnp.where(theirs < -side, theirs + box, theirs))
-            excess = jnp.maximum(jnp.abs(theirs) - 0.5 * side, 0.0)
-            beyond = beyond + excess * excess
-            planes.append(theirs)
-        keep = (beyond < REACH * REACH) & (beyond > 0.0)
-        front, held = prefix_counts(keep)
+            places.append(theirs)
+            if axis < 2:
+                excess = jnp.maximum(jnp.abs(theirs) - 0.5 * side, 0.0)
+                across = across + excess * excess
+        height = places[2]
+        outside = (across > 0.0) | (jnp.abs(height) > 0.5 * side)
         lanes = iota((8, width), 1, jnp.int32)
-        hops = jnp.where(keep, lanes - front.astype(jnp.int32), 0)
+        lists = []
+        for sign in (1.0, -1.0):
+            tilted = sign * height
+            excess = jnp.minimum(jnp.maximum(jnp.abs(tilted + 0.25 * side) - 0.25 * side, 0.0), 1.5 * side - tilted)
+            keep = outside & (across + excess * excess < REACH * REACH)
+            front, held = prefix_counts(keep)
+            lists.append((jnp.where(keep, lanes - front.astype(jnp.int32), 0), places, held.astype(jnp.int32)))
 
         slots = iota((LANES, MIG), 0)
-        done = 0
-        for bit in range(10 if width > 512 else 9):
+        starts = range(0, half_width, LANES)
+        for bit in range(0, 10, 2):
             step = 1 << bit
-            coming = pltpu.roll(hops, width - step, 1)
-            take = (coming & step) != 0
-            leave = (hops & step) != 0
-            hops = jnp.where(take, coming, jnp.where(leave, 0, hops))
-            planes = [jnp.where(take, pltpu.roll(plane, width - step, 1), plane) for plane in planes]
-            if done < width:
-                out = lax.dot_general(pieces, as_bf16(slots == slot - float(done)), NT, preferred_element_type=jnp.float32)
-                rows_ref[:, done:done + LANES] = own_ref[0:8, done:done + LANES] + sum_groups(out, 8)
-                done += LANES
-        if width < PAD:
-            rows_ref[:, width:PAD] = jnp.zeros((8, PAD - width), jnp.float32)
-
-        rows = rows_ref[:, 0:width]
+            for half in range(2):
+                hops, planes, held = lists[half]
+                next_hops = jnp.where(((hops >> bit) & 3) != 0, 0, hops)
+                moved = planes
+                for times in range(1, 4):
+                    back = width - times * step
+                    if back > 0:
+                        coming = pltpu.roll(hops, back, 1)
+                        take = ((coming >> bit) & 3) == times
+                        next_hops = jnp.where(take, coming, next_hops)
+                        moved = [jnp.where(take, pltpu.roll(old, back, 1), new) for old, new in zip(planes, moved)]
+                lists[half] = (next_hops, moved, held)
+                for start in starts[bit // 2::5]:
+                    out = lax.dot_general(pieces, as_bf16(slots == targets[half] - float(start)), NT, preferred_element_type=jnp.float32)
+                    dense_ref[half, :, start:start + LANES] = own_ref[8 * half:8 * half + 8, start:start + LANES] + sum_groups(out, 8)
+        dense_ref[0, :, half_width:PAD + LANES] = jnp.zeros((8, PAD + LANES - half_width), jnp.float32)
+        dense_ref[1, :, half_width:half_width + LANES] = jnp.zeros((8, LANES), jnp.float32)
+        lay(dense_ref.at[0], dense_ref[1, :, 0:half_width + LANES], split)
+        rows_ref[...] = dense_ref[0, :, 0:PAD]
+
+        rows = rows_ref[:, 0:slots_width]
         filled = rows[6:7, :] > 0.5
         local = rows[0:3, :] - axis_column(centre, 3)
-        near_ref[0:3, 0:width] = jnp.where(filled, local, FAR_AWAY)
-        local = jnp.concatenate([jnp.where(filled, local, -FAR_AWAY), jnp.zeros((5, width), jnp.float32)], axis=0)
+        for half in range(2):
+            near_ref[half, 0:3, 0:slots_width] = jnp.where(filled, local, FAR_AWAY)
+        local = jnp.concatenate([jnp.where(filled, local, -FAR_AWAY), jnp.zeros((5, slots_width), jnp.float32)], axis=0)
         spread = as_bf16(iota((24, 3 * LANES), 0, jnp.int32) % 8 == iota((24, 3 * LANES), 1, jnp.int32) // LANES)
         columns = lax.dot_general(pieces_of(local), spread, (((0,), (0,)), ((), ())), preferred_element_type=jnp.float32)
         for axis in range(3):
-            mine_ref[axis, 0:width, :] = columns[:, LANES * axis:LANES * (axis + 1)]
-
-        for relation in range(8):
-            for axis in range(3):
-                list_ref[relation, axis:axis + 1, 0:width] = planes[axis][relation:relation + 1, :]
-        held = held.astype(jnp.int32)
-        lane128 = iota((8, LANES), 1, jnp.int32)
-        start = total
-        for relation in range(8):
-            into = start % LANES
-            first = pl.multiple_of(start - into, LANES)
-            turned = pltpu.roll(list_ref[relation, :, 0:width + LANES], into, 1)
-            near_ref[:, pl.ds(first, LANES)] = jnp.where(lane128 < into, near_ref[:, pl.ds(first, LANES)], turned[:, 0:LANES])
-            near_ref[:, pl.ds(pl.multiple_of(first + LANES, LANES), width)] = turned[:, LANES:]
-            start = start + held[relation, 0]
-        into = start % LANES
-        first = pl.multiple_of(start - into, LANES)
-        near_ref[:, pl.ds(first, LANES)] = jnp.where(lane128 < into, near_ref[:, pl.ds(first, LANES)], FAR_AWAY)
-        count_ref[0] = (start + LANES - 1) // LANES
+            mine_ref[axis, 0:slots_width, :] = columns[:, LANES * axis:LANES * (axis + 1)]
+
+        for half in range(2):
+            _, planes, held = lists[half]
+            for relation in range(8):
+                for axis in range(3):
+                    list_ref[half, relation, axis:axis + 1, 0:width] = planes[axis][relation:relation + 1, :]
+            start = total
+            for relation in range(8):
+                lay(near_ref.at[half], list_ref[half, relation, :, 0:width + LANES], start)
+                start = start + held[relation, 0]
+            lay(near_ref.at[half], jnp.full((8, 2 * LANES), FAR_AWAY, jnp.float32), start)
+            count_ref[half] = (start + LANES - 1) // LANES
 
     @pl.when(narrow)
     def _():
-        prepare(NARROW)
+        prepare(NARROW, NARROW - LANES, NARROW + LANES)
 
     @pl.when(jnp.logical_not(narrow))
     def _():
-        prepare(PAD)
-
-    n_other = count_ref[0]
+        prepare(PAD, PAD, PAD)
+
     n_own = (total + IC - 1) // IC
 
     def sweep(span):
         def own_step(i, totals):
             first = pl.multiple_of(i * IC, IC)
+            half = (first >= split).astype(jnp.int32)
+            n_other = count_ref[half]
             own = [mine_ref[axis, pl.ds(first, IC), :] for axis in range(3)]
 
             def other_block(first, sums):
                 forces, totals = sums
-                other = [near_ref[axis:axis + 1, pl.ds(first, LANES)] for axis in range(3)]
+                other = [near_ref[half, axis:axis + 1, pl.ds(first, LANES)] for axis in range(3)]
                 force, parts = pair_terms(own, other, span)
                 forces = tuple(f + t for f, t in zip(forces, force))
                 totals = tuple(t + sum_groups(p, 8) for t, p in zip(totals, parts))
@@ -377,7 +404,7 @@
 
     exchange = pl.pallas_call(
         exchange_kernel,
-        out_shape=(shape((9, PAD)), shape((8, 1, 3 * PAD)), shape((8, 8, MIG))),
+        out_shape=(shape((17, PAD)), shape((8, 1, 3 * PAD)), shape((8, 8, MIG))),
         in_specs=[hbm] * 5 + [pl.BlockSpec(memory_space=pl.ANY)],
         out_specs=(vmem, vmem, vmem),
         scratch_shapes=[pltpu.VMEM((3, CAP), f32)] * 3 + [pltpu.VMEM((CAP,), i32)] * 2 + [pltpu.VMEM((1, 1), f32), pltpu.VMEM((9, PAD), f32), pltpu.SemaphoreType.DMA((6,)), pltpu.SemaphoreType.DMA((2, 8)), pltpu.SemaphoreType.DMA((2, 8))],
@@ -389,7 +416,7 @@
         out_shape=(shape((1, 128)), shape((3, PAD, 128)), shape((8, PAD))),
         in_specs=[vmem] * 3,
         out_specs=(vmem,) * 3,
-        scratch_shapes=[pltpu.VMEM((8, 9 * PAD + 256), f32), pltpu.VMEM((3, PAD, 128), f32), pltpu.VMEM((3, 8, PAD), f32), pltpu.VMEM((8, 8, PAD + 128), f32), pltpu.SMEM((1,), i32)],
+        scratch_shapes=[pltpu.VMEM((2, 8, 9 * PAD + 256), f32), pltpu.VMEM((3, PAD, 128), f32), pltpu.VMEM((3, 8, PAD), f32), pltpu.VMEM((2, 8, 8, PAD + 128), f32), pltpu.VMEM((2, 8, 2 * PAD + 256), f32), pltpu.SMEM((2,), i32)],
         compiler_params=pltpu.CompilerParams(vmem_limit_bytes=16 << 20),
         name="forces",
     )

time: 19.5 us -> 18.9 us (0.969)
  Pallas kernels: 17.9 us -> 17.4 us
    pallas_call x1, Pallas kernels: 4.86 us -> 3.5 us  [local_step(): partial, sums, rows = forces(own, everyone, movers)]
    pallas_call x1, Pallas kernels: 4.72 us -> 5.61 us  [local_step(): total_energy(partial, sums, rows)]
where the time goes in v2:
time: 18.9 us; the launch traced here: 18.7 us
  Pallas kernels  17.4 us (92%)
  between operations  1.3 us (7%)
    pallas_call x1, Pallas kernels, local_step(): exchange(*[pltpu.with_memory_space_constraint(array, pltpu.HBM) for array...  7.61 us
    pallas_call x1, Pallas kernels, local_step(): total_energy(partial, sums, rows)  5.61 us
    pallas_call x1, Pallas kernels, local_step(): partial, sums, rows = forces(own, everyone, movers)  3.5 us
    pallas_call x1, Pallas kernels, local_step(): store(*total_energy(partial, sums, rows))  0.67 us

profile of v2, /device:TPU:0, one launch (start us, length us, event | category | flops | bytes accessed | tf_op | source)
XLA Modules:
  0.0 18.7 jit_solution(1612740124915370644)
XLA Ops:
  1.3 7.6 %exchange.1 = (f32[17,768]{1,0:T(8,128)S(1)}, f32[8,1,2304]{2,1,0:T(1,128)S(1)}, f32[8,8,256]{2,1,0:T(8,128)S(1)}) custom-call(f32[3,729]{1,0:T(4,128)} %bitcast.9, f32[3,729]{1,0:T(4,128)} %bitcast.10, f32[3,729]{1,0:T(4,128)} %bitcast.11, s32[729]{0:T(1024)} %id_hbm.1, s32[729]{0:T(1024)} %ok_hbm.1, f32[1,1]{1,0:T(1,128)} %bitcast.8.side_hbm), custom_call_target="tpu_custom_call" | custom-call | tf_op jit(solution)/shard_map/exchange/pallas_call | solution.py:445
  8.9 3.5 %forces.1 = (f32[1,128]{1,0:T(1,128)S(1)}, f32[3,768,128]{2,1,0:T(8,128)S(1)}, f32[8,768]{1,0:T(8,128)S(1)}) custom-call(f32[17,768]{1,0:T(8,128)S(1)} %get-tuple-element.24.own_ref, f32[8,1,2304]{2,1,0:T(1,128)S(1)} %get-tuple-element.25.all_ref, f32[8,8,256]{2,1,0:T(8,128)S(1)} %get-tuple-element.26.mig_ref), custom_call_target="tpu_custom_call" | custom-call | tf_op jit(solution)/shard_map/forces/pallas_call | solution.py:446
  12.4 5.6 %energy.1 = (f32[1,128]{1,0:T(1,128)S(1)}, f32[3,729]{1,0:T(4,128)S(1)}, f32[3,729]{1,0:T(4,128)S(1)}, f32[3,729]{1,0:T(4,128)S(1)}, s32[729]{0:T(1024)S(1)}, /*index=5*/s32[729]{0:T(1024)S(1)}) custom-call(f32[1,128]{1,0:T(1,128)S(1)} %get-tuple-element.27.en_ref, f32[3,768,128]{2,1,0:T(8,128)S(1)} %get-tuple-element.28.acc_ref, ...), custom_call_target="tpu_custom_call" | custom-call | tf_op jit(solution)/shard_map/energy/pallas_call | solution.py:447
  18.0 0.7 %store.1 = (f32[3,729]{1,0:T(4,128)}, f32[3,729]{1,0:T(4,128)}, f32[3,729]{1,0:T(4,128)}, s32[729]{0:T(1024)}, s32[729]{0:T(1024)}, /*index=5*/f32[1,1]{1,0:T(1,128)}) custom-call(f32[1,128]{1,0:T(1,128)S(1)} %get-tuple-element.30.sum_ref, f32[3,729]{1,0:T(4,128)S(1)} %get-tuple-element.31.refs_0_, f32[3,729]{1,0:T(4,128)S(1)} %get-tuple-element.32.refs_1_, ...), custom_call_target="tpu_custom_call" | custom-call | tf_op jit(solution)/shard_map/store/pallas_call | solution.py:447

commit v3 on v2

--- a/solution.py
+++ b/solution.py
@@ -220,7 +220,7 @@
         pltpu.store(target.at[:, pl.ds(first, LANES)], turned[:, 0:LANES], mask=behind)
         target[:, pl.ds(pl.multiple_of(first + LANES, LANES), rows.shape[1] - LANES)] = turned[:, LANES:]
 
-    def prepare(width, half_width, slots_width):
+    def classify(width):
         for relation in range(8):
             for axis in range(3):
                 plane_ref[axis, relation:relation + 1, 0:width] = all_ref[relation, :, PAD * axis:PAD * axis + width]
@@ -243,7 +243,9 @@
             keep = outside & (across + excess * excess < REACH * REACH)
             front, held = prefix_counts(keep)
             lists.append((jnp.where(keep, lanes - front.astype(jnp.int32), 0), places, held.astype(jnp.int32)))
-
+        return lists
+
+    def prepare(lists, width, half_width, slots_width):
         slots = iota((LANES, MIG), 0)
         starts = range(0, half_width, LANES)
         for bit in range(0, 10, 2):
@@ -291,13 +293,15 @@
             lay(near_ref.at[half], jnp.full((8, 2 * LANES), FAR_AWAY, jnp.float32), start)
             count_ref[half] = (start + LANES - 1) // LANES
 
+    short_lists = classify(NARROW)
+
     @pl.when(narrow)
     def _():
-        prepare(NARROW, NARROW - LANES, NARROW + LANES)
+        prepare(short_lists, NARROW, NARROW - LANES, NARROW + LANES)
 
     @pl.when(jnp.logical_not(narrow))
     def _():
-        prepare(PAD, PAD, PAD)
+        prepare(classify(PAD), PAD, PAD, PAD)
 
     n_own = (total + IC - 1) // IC
 

time: 18.9 us -> 19 us (level)
    pallas_call x1, Pallas kernels: 3.5 us -> 4.57 us  [local_step(): partial, sums, rows = forces(own, everyone, movers)]
    pallas_call x1, Pallas kernels: 5.61 us -> 4.67 us  [local_step(): total_energy(partial, sums, rows)]
where the time goes in v3:
time: 19 us; the launch traced here: 18.8 us
  Pallas kernels  17.5 us (92%)
  between operations  1.3 us (7%)
    pallas_call x1, Pallas kernels, local_step(): exchange(*[pltpu.with_memory_space_constraint(array, pltpu.HBM) for array...  7.61 us
    pallas_call x1, Pallas kernels, local_step(): total_energy(partial, sums, rows)  4.67 us
    pallas_call x1, Pallas kernels, local_step(): partial, sums, rows = forces(own, everyone, movers)  4.57 us
    pallas_call x1, Pallas kernels, local_step(): store(*total_energy(partial, sums, rows))  0.67 us

profile of v3, /device:TPU:0, one launch (start us, length us, event | category | flops | bytes accessed | tf_op | source)
XLA Modules:
  0.0 18.8 jit_solution(1137920175861870085)
XLA Ops:
  1.3 7.6 %exchange.1 = (f32[17,768]{1,0:T(8,128)S(1)}, f32[8,1,2304]{2,1,0:T(1,128)S(1)}, f32[8,8,256]{2,1,0:T(8,128)S(1)}) custom-call(f32[3,729]{1,0:T(4,128)} %bitcast.9, f32[3,729]{1,0:T(4,128)} %bitcast.10, f32[3,729]{1,0:T(4,128)} %bitcast.11, s32[729]{0:T(1024)} %id_hbm.1, s32[729]{0:T(1024)} %ok_hbm.1, f32[1,1]{1,0:T(1,128)} %bitcast.8.side_hbm), custom_call_target="tpu_custom_call" | custom-call | tf_op jit(solution)/shard_map/exchange/pallas_call | solution.py:449
  8.9 4.6 %forces.1 = (f32[1,128]{1,0:T(1,128)S(1)}, f32[3,768,128]{2,1,0:T(8,128)S(1)}, f32[8,768]{1,0:T(8,128)S(1)}) custom-call(f32[17,768]{1,0:T(8,128)S(1)} %get-tuple-element.24.own_ref, f32[8,1,2304]{2,1,0:T(1,128)S(1)} %get-tuple-element.25.all_ref, f32[8,8,256]{2,1,0:T(8,128)S(1)} %get-tuple-element.26.mig_ref), custom_call_target="tpu_custom_call" | custom-call | tf_op jit(solution)/shard_map/forces/pallas_call | solution.py:450
  13.5 4.7 %energy.1 = (f32[1,128]{1,0:T(1,128)S(1)}, f32[3,729]{1,0:T(4,128)S(1)}, f32[3,729]{1,0:T(4,128)S(1)}, f32[3,729]{1,0:T(4,128)S(1)}, s32[729]{0:T(1024)S(1)}, /*index=5*/s32[729]{0:T(1024)S(1)}) custom-call(f32[1,128]{1,0:T(1,128)S(1)} %get-tuple-element.27.en_ref, f32[3,768,128]{2,1,0:T(8,128)S(1)} %get-tuple-element.28.acc_ref, ...), custom_call_target="tpu_custom_call" | custom-call | tf_op jit(solution)/shard_map/energy/pallas_call | solution.py:451
  18.2 0.7 %store.1 = (f32[3,729]{1,0:T(4,128)}, f32[3,729]{1,0:T(4,128)}, f32[3,729]{1,0:T(4,128)}, s32[729]{0:T(1024)}, s32[729]{0:T(1024)}, /*index=5*/f32[1,1]{1,0:T(1,128)}) custom-call(f32[1,128]{1,0:T(1,128)S(1)} %get-tuple-element.30.sum_ref, f32[3,729]{1,0:T(4,128)S(1)} %get-tuple-element.31.refs_0_, f32[3,729]{1,0:T(4,128)S(1)} %get-tuple-element.32.refs_1_, ...), custom_call_target="tpu_custom_call" | custom-call | tf_op jit(solution)/shard_map/store/pallas_call | solution.py:451

commit v4 on v3

--- a/solution.py
+++ b/solution.py
@@ -291,7 +291,7 @@
                 lay(near_ref.at[half], list_ref[half, relation, :, 0:width + LANES], start)
                 start = start + held[relation, 0]
             lay(near_ref.at[half], jnp.full((8, 2 * LANES), FAR_AWAY, jnp.float32), start)
-            count_ref[half] = (start + LANES - 1) // LANES
+            count_ref[half] = (start + 2 * LANES - 1) // (2 * LANES)
 
     short_lists = classify(NARROW)
 
@@ -324,12 +324,8 @@
                 first = pl.multiple_of(j * 2 * LANES, 2 * LANES)
                 return other_block(first + LANES, other_block(first, sums))
 
-            def last_step(j, sums):
-                return other_block(pl.multiple_of((n_other - 1) * LANES, LANES), sums)
-
             zero = jnp.zeros((IC, LANES), jnp.float32)
-            sums = lax.fori_loop(0, n_other // 2, other_step, ((zero,) * 3, totals))
-            forces, totals = lax.fori_loop(0, n_other % 2, last_step, sums)
+            forces, totals = lax.fori_loop(0, n_other, other_step, ((zero,) * 3, totals))
             for axis in range(3):
                 acc_ref[axis, pl.ds(first, IC), :] = forces[axis]
             return totals

time: 19 us -> 18.3 us (0.963)
  Pallas kernels: 17.5 us -> 16.7 us
    pallas_call x1, Pallas kernels: 4.57 us -> 3.2 us  [local_step(): partial, sums, rows = forces(own, everyone, movers)]
    pallas_call x1, Pallas kernels: 4.67 us -> 5.21 us  [local_step(): total_energy(partial, sums, rows)]
where the time goes in v4:
time: 18.3 us; the launch traced here: 18 us
  Pallas kernels  16.7 us (91%)
  between operations  1.3 us (7%)
    pallas_call x1, Pallas kernels, local_step(): exchange(*[pltpu.with_memory_space_constraint(array, pltpu.HBM) for array...  7.61 us
    pallas_call x1, Pallas kernels, local_step(): total_energy(partial, sums, rows)  5.21 us
    pallas_call x1, Pallas kernels, local_step(): partial, sums, rows = forces(own, everyone, movers)  3.2 us
    pallas_call x1, Pallas kernels, local_step(): store(*total_energy(partial, sums, rows))  0.67 us

profile of v4, /device:TPU:0, one launch (start us, length us, event | category | flops | bytes accessed | tf_op | source)
XLA Modules:
  0.0 18.0 jit_solution(1216466570226350171)
XLA Ops:
  1.3 7.6 %exchange.1 = (f32[17,768]{1,0:T(8,128)S(1)}, f32[8,1,2304]{2,1,0:T(1,128)S(1)}, f32[8,8,256]{2,1,0:T(8,128)S(1)}) custom-call(f32[3,729]{1,0:T(4,128)} %bitcast.9, f32[3,729]{1,0:T(4,128)} %bitcast.10, f32[3,729]{1,0:T(4,128)} %bitcast.11, s32[729]{0:T(1024)} %id_hbm.1, s32[729]{0:T(1024)} %ok_hbm.1, f32[1,1]{1,0:T(1,128)} %bitcast.8.side_hbm), custom_call_target="tpu_custom_call" | custom-call | tf_op jit(solution)/shard_map/exchange/pallas_call | solution.py:445
  8.9 3.2 %forces.1 = (f32[1,128]{1,0:T(1,128)S(1)}, f32[3,768,128]{2,1,0:T(8,128)S(1)}, f32[8,768]{1,0:T(8,128)S(1)}) custom-call(f32[17,768]{1,0:T(8,128)S(1)} %get-tuple-element.24.own_ref, f32[8,1,2304]{2,1,0:T(1,128)S(1)} %get-tuple-element.25.all_ref, f32[8,8,256]{2,1,0:T(8,128)S(1)} %get-tuple-element.26.mig_ref), custom_call_target="tpu_custom_call" | custom-call | tf_op jit(solution)/shard_map/forces/pallas_call | solution.py:446
  12.1 5.2 %energy.1 = (f32[1,128]{1,0:T(1,128)S(1)}, f32[3,729]{1,0:T(4,128)S(1)}, f32[3,729]{1,0:T(4,128)S(1)}, f32[3,729]{1,0:T(4,128)S(1)}, s32[729]{0:T(1024)S(1)}, /*index=5*/s32[729]{0:T(1024)S(1)}) custom-call(f32[1,128]{1,0:T(1,128)S(1)} %get-tuple-element.27.en_ref, f32[3,768,128]{2,1,0:T(8,128)S(1)} %get-tuple-element.28.acc_ref, ...), custom_call_target="tpu_custom_call" | custom-call | tf_op jit(solution)/shard_map/energy/pallas_call | solution.py:447
  17.3 0.7 %store.1 = (f32[3,729]{1,0:T(4,128)}, f32[3,729]{1,0:T(4,128)}, f32[3,729]{1,0:T(4,128)}, s32[729]{0:T(1024)}, s32[729]{0:T(1024)}, /*index=5*/f32[1,1]{1,0:T(1,128)}) custom-call(f32[1,128]{1,0:T(1,128)S(1)} %get-tuple-element.30.sum_ref, f32[3,729]{1,0:T(4,128)S(1)} %get-tuple-element.31.refs_0_, f32[3,729]{1,0:T(4,128)S(1)} %get-tuple-element.32.refs_1_, ...), custom_call_target="tpu_custom_call" | custom-call | tf_op jit(solution)/shard_map/store/pallas_call | solution.py:447
